TPU v7x, 16 devices: a whole 2x2x2 slice. The times are simulated.
16 devices in a mesh: dp: 1, sp: 16 (over x, y, z, core).
Axes of the slice: x: 2, y: 2, z: 2, core: 2. Of those that a mesh axis runs over, the one named last changes fastest.
Arguments:
- q: bfloat16 [32, 16, 128], P('dp')
- k: bfloat16 [32, 8192, 16, 128], P('dp', 'sp')
- v: bfloat16 [32, 8192, 16, 128], P('dp', 'sp')
Outputs:
- q: bfloat16 [32, 16, 128], P('dp')
All inputs are finite; a program needn't handle non-finite values.
Results may differ from a plain program's by a relative error of at most 0.012.
Values are sent between devices in bfloat16 or wider.
A program may use at most 2 GiB of HBM per device.

v0:
```python
import jax
import jax.numpy as jnp
from jax import lax
from jax.sharding import PartitionSpec as P


def einsum(form, a, b):
    return jnp.einsum(form, a.astype(jnp.float32), b.astype(jnp.float32))


def part_of(q, k, v):
    grouped = q.reshape(q.shape[0], k.shape[2], -1, q.shape[2])
    scores = einsum("bgsd,bugd->bgsu", grouped, k) * q.shape[2] ** -0.5
    high = jnp.max(scores, -1, keepdims=True)
    weights = jnp.exp(scores - high)
    seen = einsum("bgsu,bugd->bgsd", weights.astype(jnp.bfloat16), v)
    return jnp.concatenate([seen, jnp.sum(weights, -1, keepdims=True), high], -1)


def together(parts):
    seen, total, high = parts[..., :-2], parts[..., -2:-1], parts[..., -1:]
    scale = jnp.exp(high - jnp.max(high, 0))
    return (jnp.sum(seen * scale, 0) / jnp.sum(total * scale, 0)).astype(jnp.bfloat16)


def solution(mesh):
    def step(q, k, v):
        return together(lax.all_gather(part_of(q, k, v), "sp")).reshape(q.shape)

    return jax.shard_map(
        step,
        mesh=mesh,
        in_specs=(P("dp", None, None), P("dp", "sp", None, None), P("dp", "sp", None, None)),
        out_specs=P("dp", None, None),
        check_vma=False,
    )
```

profile of v0, /device:TPU:0, one launch (start us, length us, event | category | flops | bytes accessed | tf_op | source)
XLA Modules:
  0.0 150.1 jit_solution(4371463910500022071)
XLA Ops:
  6.5 0.0 all-gather.3.cloned.1.call-start
  6.5 31.9 %fusion.2 = f32[32,16,1,512]{3,2,1,0:T(1,128)S(1)} fusion(bf16[32,512,16,128]{3,2,1,0:T(8,128)(2,1)} %param.4, bf16[32,16,128,1]{2,1,0,3:T(8,128)(2,1)} %bitcast.25), kind=kOutput, calls=%fused_computation.2 | convolution fusion | flops 67108864 | bytes 68288512 | tf_op jit(solution)/shard_map/bgsd,bugd->bgsu/dot_general | solution.py:8
  38.5 0.2 fusion.9
  38.6 0.3 fusion.10
  39.0 0.3 copy.23
  39.2 0.3 copy.22
  39.5 32.6 %fusion = f32[32,16,1,128]{3,2,1,0:T(1,128)S(1)} fusion(bf16[32,512,16,128]{3,2,1,0:T(8,128)(2,1)} %param.5, bf16[32,16,512,1]{2,1,0,3:T(8,128)(2,1)S(1)} %get-tuple-element.7), kind=kOutput, calls=%fused_computation | convolution fusion | flops 67108864 | bytes 67895296 | tf_op jit(solution)/shard_map/bgsu,bugd->bgsd/dot_general | solution.py:8
  72.1 1.0 pad_maximum_fusion
  73.1 0.0 all-gather.3.cloned.1.call-update
  73.1 51.6 %all-gather.3.cloned.1.call-done = f32[512,16,1,130]{3,1,2,0:T(8,128)} async-done(((f32[32,16,1,130]{3,1,2,0:T(8,128)}), f32[512,16,1,130]{3,1,2,0:T(8,128)}) %all-gather.3.cloned.1.call-update) | async-done | bytes 4259856 | tf_op jit(solution)/shard_map/all_gather | solution.py:28
  124.8 3.4 %slice_reduce_fusion = f32[32,16]{1,0:T(8,128)S(1)} fusion(f32[16,32,16,1,130]{4,2,1,0,3:T(8,128)} %bitcast.21), kind=kLoop, calls=%fused_computation.9 | loop fusion | flops 7680 | bytes 34816 | tf_op jit(solution)/shard_map/reduce_max | solution.py:22
  128.2 6.7 %fusion.4 = (f32[32,16]{1,0:T(8,128)S(1)}, f32[16,32,16,1,1]{4,2,1,0,3:T(8,128)}) fusion(f32[16,32,16,1,130]{4,2,1,0,3:T(8,128)} %bitcast.22, f32[32,16]{1,0:T(8,128)S(1)} %slice_reduce_fusion), kind=kLoop, calls=%fused_computation.5 | loop fusion | flops 24064 | bytes 102400 | tf_op jit(solution)/shard_map/reduce_sum | solution.py:23
  134.9 4.7 %copy.36 = f32[16,32,16,1,1]{2,1,0,3,4:T(8,128)S(1)} copy(f32[16,32,16,1,1]{4,2,1,0,3:T(8,128)} %get-tuple-element.6) | data formatting | bytes 65536 | tf_op jit(solution)/shard_map/mul | solution.py:23
  139.6 2.9 %fusion.5 = f32[32,16,128]{2,1,0:T(8,128)S(1)} fusion(f32[16,32,16,1,130]{4,2,1,0,3:T(8,128)} %bitcast.23, f32[16,32,16]{2,1,0:T(8,128)S(1)} %bitcast.24), kind=kLoop, calls=%fused_computation.7 | loop fusion | flops 2031616 | bytes 4489216 | tf_op jit(solution)/shard_map/reduce_sum | solution.py:23
  142.5 0.8 divide_convert_fusion
Async XLA Ops:
  6.5 118.2 %all-gather.3.cloned.1.call-start = ((), (), s32[]{:S(2)}) async-start(), calls=%async_computation | async-start | bytes 8912896 | tf_op jit(solution)/shard_map/all_gather | solution.py:28
Sparse Core Ops, SparseCore 0:
  73.2 51.4 all-gather.2
where the time goes:
time: 150 us
  matrix products  64.5 us (43%)
  waiting for transfers between devices  51.6 us (34%)
  other arithmetic  15.3 us (10%)
  between operations  13.4 us (9%)
  local copies, waits for them, and re-layouts  5.22 us (3%)
    dot_general x2, matrix products, einsum(): return jnp.einsum(form, a.astype(jnp.float32), b.astype(jnp.float32))  64.5 us
    all_gather x1, waiting for transfers between devices, step(): return together(lax.all_gather(part_of(q, k, v), 'sp')).reshape(q.shape)  51.6 us
    reduce_sum x1, other arithmetic, together(): jnp.sum(total * scale, 0)  6.67 us
    mul x1, local copies, waits for them, and re-layouts, together(): seen * scale  4.69 us
    reduce_max x1, other arithmetic, together(): scale = jnp.exp(high - jnp.max(high, 0))  3.42 us
  transfers between devices with their start and end apart: 1, of which 1 were waited for; matrix products, arithmetic and copies ran while one was open for 0% of the time, Pallas kernels for 0%

commit v1 on v0

v1 whole, which is shorter than its diff:
```python
import functools, math
import jax, jax.numpy as jnp
from jax import lax
from jax.experimental import pallas as pl
from jax.experimental.pallas import tpu as pltpu
from jax.sharding import PartitionSpec as P

LOG2E = math.log2(math.e)
SLOTS = 4
MODE = "full"
SCALE = 128 ** -0.5 * LOG2E

def scores(w_ref, k):
    k4 = k.reshape(32, 8, 16, 128)
    lhs = jnp.concatenate([k4[:, t].reshape(512, 128) for t in range(8)], -1)
    s = lax.dot_general(lhs, w_ref[...], (((1,), (1,)), ((), ())), preferred_element_type=jnp.float32)
    return s.reshape(32, 16, 128)

def weigh(s, scale):
    row = lax.broadcasted_iota(jnp.int32, (16, 128), 0)
    col = lax.broadcasted_iota(jnp.int32, (16, 128), 1)
    mask = lax.rem(col, 16) == row
    top = jnp.max(s, 0)
    high = jnp.max(jnp.where(mask, top, -jnp.inf), -1, keepdims=True)
    p = jnp.where(mask[None], jnp.exp2(s * scale - high * scale), 0.0)
    total = jnp.sum(jnp.sum(p, 0), -1, keepdims=True)
    return p.astype(jnp.bfloat16), high, total

def mix(p, v):
    v2 = v.reshape(2, 2048, 128)
    rhs = jnp.concatenate([v2[0], v2[1]], -1)
    a = jnp.concatenate([p[g] for g in range(16)], -1)
    b = jnp.concatenate([p[g] for g in range(16, 32)], -1)
    lhs = jnp.concatenate([a, b], 0)
    r = jnp.dot(lhs, rhs, preferred_element_type=jnp.float32)
    return r[:16, :128] + r[16:, 128:]

MESH = pl.DeviceIdType.MESH
GROUP = 4


def combine(racc, rst, o_ref, b):
    rows = rst[:, b]
    top = jnp.max(rows, 0, keepdims=True)
    scale = jnp.exp2((rows - top) * SCALE)
    sums = pltpu.roll(rows, 112, 2)
    w = scale / jnp.sum(scale * sums, 0, keepdims=True)
    head = lax.broadcasted_iota(jnp.int32, (16, 128), 0)
    lane = lax.broadcasted_iota(jnp.int32, (16, 128), 1)
    pick = head == lane
    out = jnp.zeros((16, 128), jnp.float32)
    for d in range(16):
        col = jnp.sum(jnp.where(pick, jnp.broadcast_to(w[d], (16, 128)), 0.0), -1, keepdims=True)
        out = out + racc[d, b].astype(jnp.float32) * col
    o_ref[b] = out.astype(jnp.bfloat16)


def kernel(q_ref, k_hbm, v_hbm, o_ref, kbuf, vbuf, w_ref, s0, s1, p0, p1, st0, st1, racc, rst, ksem, vsem, asend, arecv, ssend, srecv):
    n = q_ref.shape[0]
    parts = racc.shape[0]
    bulk = n // GROUP - 1
    me = lax.axis_index("sp")
    s_refs, p_refs, st = (s0, s1), (p0, p1), (st0, st1)
    def kcopy(b):
        s = lax.rem(b, SLOTS)
        return pltpu.make_async_copy(k_hbm.at[b], kbuf.at[s], ksem.at[s])
    def vcopy(b):
        s = lax.rem(b, SLOTS)
        return pltpu.make_async_copy(v_hbm.at[b], vbuf.at[s], vsem.at[s])
    for b in range(SLOTS):
        kcopy(b).start(); vcopy(b).start()

    barrier = pltpu.get_barrier_semaphore()
    def peer(i):
        return {"sp": lax.rem(me + i, parts)}
    def greet(i, c):
        pl.semaphore_signal(barrier, inc=1, device_id=peer(i), device_id_type=MESH)
        return c
    lax.fori_loop(1, parts, greet, 0)
    w_ref[...] = jnp.zeros_like(w_ref)

    def copies(slot, start, size, g, i):
        seqs = pl.ds(start, size)
        return (
            pltpu.make_async_remote_copy(racc.at[slot, seqs], racc.at[slot, seqs], asend.at[g], arecv.at[g], device_id=peer(i), device_id_type=MESH),
            pltpu.make_async_remote_copy(rst.at[slot, seqs], rst.at[slot, seqs], ssend.at[g], srecv.at[g], device_id=peer(i), device_id_type=MESH),
        )
    def send(start, size, g):
        for i in range(1, parts):
            for c in copies(me, start, size, g, i):
                c.start()
    def arrived(start, size, g):
        for c in copies(pl.ds(0, parts - 1), start, size, g, 1):
            c.wait_recv()
    def sent(start, size, g):
        for c in copies(pl.ds(0, parts - 1), start, size, g, 1):
            c.wait_send()
    def fill(b):
        for j in range(8):
            w_ref[16*j:16*j+16, 128*j:128*j+128] = q_ref[b]
    def qk(b, h):
        s_refs[h][...] = scores(w_ref, kbuf[lax.rem(b, SLOTS), 256*h:256*h+256])
    def wt(h):
        p, high, total = weigh(s_refs[h][...], SCALE)
        p_refs[h][...] = p
        st[h][0] = jnp.broadcast_to(high, (16, 128))
        st[h][1] = jnp.broadcast_to(total, (16, 128))
    def pv(b, h):
        return mix(p_refs[h][...], vbuf[lax.rem(b, SLOTS), 256*h:256*h+256])
    def finish(b, o0, o1, h0, t0):
        h1, t1 = st[1][0], st[1][1]
        top = jnp.maximum(h0, h1)
        c0, c1 = jnp.exp2((h0 - top) * SCALE), jnp.exp2((h1 - top) * SCALE)
        racc[me, b] = (o0 * c0 + o1 * c1).astype(jnp.bfloat16)
        t = t0 * c0 + t1 * c1
        head = lax.broadcasted_iota(jnp.int32, (16, 128), 0)
        lane = lax.broadcasted_iota(jnp.int32, (16, 128), 1)
        rst[me, b] = jnp.sum(jnp.where(lane == head, top, jnp.where(lane == head + 16, t, 0.0)), 0, keepdims=True)

    def body(b, c):
        kcopy(b).wait()
        vcopy(b - 1).wait()
        fill(b)
        h0, t0 = st[0][0], st[0][1]
        o0 = pv(b - 1, 0)
        wt(1)
        qk(b, 0)
        o1 = pv(b - 1, 1)
        finish(b - 1, o0, o1, h0, t0)
        wt(0)
        qk(b, 1)
        @pl.when(b + SLOTS < n)
        def _():
            kcopy(b + SLOTS).start()
        @pl.when(b - 1 + SLOTS < n)
        def _():
            vcopy(b - 1 + SLOTS).start()
        @pl.when(b == GROUP)
        def _():
            pl.semaphore_wait(barrier, parts - 1)
        @pl.when((lax.rem(b, GROUP) == 0) & (b <= bulk * GROUP))
        def _():
            send(b - GROUP, GROUP, b // GROUP - 1)
        @pl.when((lax.rem(b, GROUP) == 0) & (b >= 2 * GROUP))
        def _():
            g = b // GROUP - 2
            arrived(g * GROUP, GROUP, g)
            for i in range(GROUP):
                combine(racc, rst, o_ref, g * GROUP + i)
        @pl.when(b == n - 2)
        def _():
            send(n - 4, 2, bulk)
        @pl.when(b == n - 1)
        def _():
            send(n - 2, 1, bulk + 1)
        return c
    kcopy(0).wait()
    fill(0)
    qk(0, 0)
    wt(0)
    qk(0, 1)
    kcopy(SLOTS).start()
    lax.fori_loop(1, n, body, 0)
    vcopy(n - 1).wait()
    h0, t0 = st[0][0], st[0][1]
    o0 = pv(n - 1, 0)
    wt(1)
    o1 = pv(n - 1, 1)
    finish(n - 1, o0, o1, h0, t0)
    send(n - 1, 1, bulk + 2)
    last = bulk - 1
    tail = [(last * GROUP, GROUP, last), (n - 4, 2, bulk), (n - 2, 1, bulk + 1), (n - 1, 1, bulk + 2)]
    for start, size, g in tail:
        arrived(start, size, g)
        for i in range(size):
            combine(racc, rst, o_ref, start + i)
    def drain(g, c):
        sent(g * GROUP, GROUP, g)
        return c
    lax.fori_loop(0, bulk, drain, 0)
    for start, size, g in tail[1:]:
        sent(start, size, g)

def solution(mesh):
    def step(q, k, v):
        n = q.shape[0]
        return pl.pallas_call(
            kernel,
            out_shape=jax.ShapeDtypeStruct(q.shape, jnp.bfloat16),
            in_specs=[pl.BlockSpec(memory_space=pltpu.VMEM), pl.BlockSpec(memory_space=pl.ANY), pl.BlockSpec(memory_space=pl.ANY)],
            out_specs=pl.BlockSpec(memory_space=pltpu.VMEM),
            scratch_shapes=[
                pltpu.VMEM((SLOTS, 512, 16, 128), jnp.bfloat16),
                pltpu.VMEM((SLOTS, 512, 16, 128), jnp.bfloat16),
                pltpu.VMEM((128, 1024), jnp.bfloat16),
                pltpu.VMEM((32, 16, 128), jnp.float32),
                pltpu.VMEM((32, 16, 128), jnp.float32),
                pltpu.VMEM((32, 16, 128), jnp.bfloat16),
                pltpu.VMEM((32, 16, 128), jnp.bfloat16),
                pltpu.VMEM((2, 16, 128), jnp.float32),
                pltpu.VMEM((2, 16, 128), jnp.float32),
                pltpu.VMEM((16, n, 16, 128), jnp.bfloat16),
                pltpu.VMEM((16, n, 1, 128), jnp.float32),
                pltpu.SemaphoreType.DMA((SLOTS,)),
                pltpu.SemaphoreType.DMA((SLOTS,)),
                pltpu.SemaphoreType.DMA((n // GROUP + 2,)),
                pltpu.SemaphoreType.DMA((n // GROUP + 2,)),
                pltpu.SemaphoreType.DMA((n // GROUP + 2,)),
                pltpu.SemaphoreType.DMA((n // GROUP + 2,)),
            ],
            compiler_params=pltpu.CompilerParams(vmem_limit_bytes=60 * 1024 * 1024, collective_id=0, has_side_effects=True),
        )(q, k, v)
    return jax.shard_map(step, mesh=mesh,
        in_specs=(P("dp", None, None), P("dp", "sp", None, None), P("dp", "sp", None, None)),
        out_specs=P("dp", None, None), check_vma=False)
```

time: 150 us -> 53.5 us (0.36)
  matrix products: 64.5 us -> 0 us
  Pallas kernels: 0 us -> 51.7 us
  waiting for transfers between devices: 51.6 us -> 0 us
  other arithmetic: 15.3 us -> 0 us
  between operations: 13.4 us -> 0.01 us
  local copies, waits for them, and re-layouts: 5.22 us -> 1.57 us
    dot_general x2 -> x0, matrix products: 64.5 us -> none  [einsum(): return jnp.einsum(form, a.astype(jnp.float32), b.astype(jnp.float32))]
    pallas_call x0 -> x1, Pallas kernels: none -> 51.7 us  [step(): pl.pallas_call(kernel, out_shape=jax.ShapeDtypeStruct(q.shape, jnp.bfloat...]
    all_gather x1 -> x0, waiting for transfers between devices: 51.6 us -> none  [step(): return together(lax.all_gather(part_of(q, k, v), 'sp')).reshape(q.shape)]
    reduce_sum x2 -> x0, other arithmetic: 9.61 us -> none  [the longest x1 6.67 us: together(): jnp.sum(total * scale, 0)]
    mul x1 -> x0, local copies, waits for them, and re-layouts: 4.69 us -> none  [together(): seen * scale]
    reduce_max x2 -> x0, other arithmetic: 3.6 us -> none  [the longest x1 3.42 us: together(): scale = jnp.exp(high - jnp.max(high, 0))]
    unnamed x0 -> x1, local copies, waits for them, and re-layouts: none -> 1.57 us
  transfers between devices with their start and end apart: 1 -> 0, of which waited for: 1 -> 0; matrix products, arithmetic and copies ran while one was open for 0% -> 0% of each run, Pallas kernels for 0% -> 0%
where the time goes in v1:
time: 53.5 us; the launch traced here: 53.3 us
  Pallas kernels  51.7 us (97%)
  local copies, waits for them, and re-layouts  1.57 us (3%)
    pallas_call x1, Pallas kernels, step(): pl.pallas_call(kernel, out_shape=jax.ShapeDtypeStruct(q.shape, jnp.bfloat...  51.7 us
    unnamed x1, local copies, waits for them, and re-layouts  1.57 us

profile of v1, /device:TPU:0, one launch (start us, length us, event | category | flops | bytes accessed | tf_op | source)
XLA Modules:
  0.0 53.3 jit_solution(8286313526479427749)
XLA Ops:
  0.0 51.7 %shard_map.37 = bf16[32,16,128]{2,1,0:T(8,128)(2,1)} custom-call(bf16[32,16,128]{2,1,0:T(8,128)(2,1)} %q_ref.1, bf16[32,512,16,128]{3,2,1,0:T(8,128)(2,1)} %k_hbm.1, bf16[32,512,16,128]{3,2,1,0:T(8,128)(2,1)} %v_hbm.1), custom_call_target="tpu_custom_call" | custom-call | tf_op jit(solution)/shard_map/pallas_call | solution.py:187
  51.8 1.6 %copy.5 = bf16[32,16,128]{2,1,0:T(8,128)(2,1)} copy(bf16[32,16,128]{2,1,0:T(8,128)(2,1)} %shard_map.37) | data formatting | bytes 262144
